TPU v7x, 32 devices: a whole 2x2x4 slice. The times are simulated.
32 devices in a mesh: rep: 2 (over y), exp: 4 (over x, core), tp: 4 (over z).
Axes of the slice: x: 2, y: 2, z: 4, core: 2. Of those that a mesh axis runs over, the one named last changes fastest.
Arguments:
- tokens: bfloat16 [256, 6144], P(('rep', 'exp'), 'tp'), parts along dimension 0, may hold values from -6 to 6
- expert_ids: int32 [256, 2], P(('rep', 'exp')), parts along dimension 0, may hold values from 0 to 3, all different within a row; in each aligned block of 32 rows (0 to 31, 32 to 63, ...) at most 20 rows name the same one
- route_logits: float32 [256, 2], P(('rep', 'exp')), parts along dimension 0, may hold values from -6 to 6
- gate_weight: bfloat16 [6144, 32768], P(None, ('exp', 'tp')), may hold values from -0.078125 to 0.078125
- up_weight: bfloat16 [6144, 32768], P(None, ('exp', 'tp')), may hold values from -0.078125 to 0.078125
- down_weight: bfloat16 [32768, 6144], P(('exp', 'tp')), may hold values from -0.0625 to 0.0625
Outputs:
- moe_out: bfloat16 [256, 6144], P(('rep', 'exp'), 'tp'), parts along dimension 0
There are 2 independent parts, one for each index of `rep`. A program takes and returns all parts, laid end to end along the dimension named above; an argument that names none is the same for every part. Nothing has to cross between parts.
Inputs may be any that keep to these rules, and one draw needn't show every extreme that they name: `expert_ids`: each token names two different experts. In each aligned block of 32 tokens no expert is named by more than 20 tokens, a bound that some block reaches.
All inputs are finite; a program needn't handle non-finite values.
Results may differ from a plain program's by a relative error of at most 0.019.
Values may be sent and summed in bfloat16 or wider, within the bound.
A program may use at most 128 MiB of HBM per device.

v0:
```python
import jax
import jax.numpy as jnp
from jax import lax
from jax.sharding import PartitionSpec as P

D = 6144
EXPERTS = 4
CAP = 20


def slot_tables(expert_ids, route_logits):
    chosen = (expert_ids[:, :, None] == jnp.arange(EXPERTS, dtype=jnp.int32)[None, None, :]).astype(
        jnp.int32
    )
    per_token = jnp.sum(chosen, axis=1)
    before = jnp.cumsum(per_token, axis=0) - per_token
    position = jnp.sum(chosen * before[:, None, :], axis=2)
    at_slot = (position[:, :, None] == jnp.arange(CAP, dtype=jnp.int32)[None, None, :]).astype(
        jnp.float32
    )
    chosen_f = chosen.astype(jnp.float32)
    diff = route_logits[:, 0] - route_logits[:, 1]
    shares = jnp.stack([jax.nn.sigmoid(diff), jax.nn.sigmoid(-diff)], axis=1)
    placement = jnp.einsum("tke,tkc->ect", chosen_f, at_slot)
    mixing = jnp.einsum("tk,tke,tkc->tec", shares, chosen_f, at_slot)
    return (placement.astype(jnp.bfloat16), mixing)


def on_device(tokens, expert_ids, route_logits, gate_weight, up_weight, down_weight):
    exp_count = lax.axis_size("exp")
    groups = exp_count // EXPERTS
    placement, mixing = slot_tables(expert_ids, route_logits)
    whole_rows = lax.all_gather(tokens, "tp", axis=1, tiled=True)
    slots = jnp.einsum(
        "ect,td->ecd", placement, whole_rows, preferred_element_type=jnp.float32
    ).astype(jnp.bfloat16)
    outgoing = jnp.repeat(slots, groups, axis=0)
    gathered = lax.all_to_all(outgoing, "exp", split_axis=0, concat_axis=0, tiled=True)
    slot_rows = gathered.reshape(exp_count * CAP, D)
    gate_act = jnp.dot(slot_rows, gate_weight, preferred_element_type=jnp.float32)
    up_act = jnp.dot(slot_rows, up_weight, preferred_element_type=jnp.float32)
    hidden = (jax.nn.silu(gate_act) * up_act).astype(jnp.bfloat16)
    partial_value = jnp.dot(hidden, down_weight, preferred_element_type=jnp.float32).astype(
        jnp.bfloat16
    )
    partial_value = lax.optimization_barrier(partial_value).reshape(exp_count, CAP, D)
    narrow = lax.psum_scatter(
        partial_value.astype(jnp.float32).astype(jnp.bfloat16),
        "tp",
        scatter_dimension=2,
        tiled=True,
    ).astype(jnp.float32)
    returned = lax.all_to_all(
        narrow.astype(jnp.bfloat16), "exp", split_axis=0, concat_axis=0, tiled=True
    ).astype(narrow.dtype)
    summed = jnp.sum(returned.reshape(EXPERTS, groups, CAP, returned.shape[2]), axis=1)
    moe_out = jnp.einsum("tec,ecd->td", mixing, summed, precision=lax.Precision.HIGHEST).astype(
        jnp.bfloat16
    )
    return moe_out


def solution(mesh):
    return jax.shard_map(
        on_device,
        mesh=mesh,
        in_specs=(
            P(("rep", "exp"), "tp"),
            P(("rep", "exp"), None),
            P(("rep", "exp"), None),
            P(None, ("exp", "tp")),
            P(None, ("exp", "tp")),
            P(("exp", "tp"), None),
        ),
        out_specs=P(("rep", "exp"), "tp"),
        check_vma=False,
    )
```

profile of v0, /device:TPU:0, one launch (start us, length us, event | category | flops | bytes accessed | tf_op | source)
XLA Modules:
  0.0 124.6 jit_solution(4549421285769029820)
XLA Ops:
  6.5 0.0 reduce-scatter.2.cloned.1.call-start
  6.5 0.7 convert_reduce_fusion
  7.2 0.7 convert_convert_fusion
  7.9 0.1 copy.11
  8.0 0.1 reduce_window_sum.11
  8.1 0.1 copy.13
  8.1 0.7 select_reduce_fusion
  8.8 0.1 copy.14
  8.9 0.1 copy.16
  9.0 16.5 %all_gather.3 = bf16[32,6144]{1,0:T(8,128)(2,1)S(1)} all-gather(bf16[32,1536]{1,0:T(8,128)(2,1)} %param.6), channel_id=1, replica_groups=mesh['rep'=2,'exp'=4,'tp'=4] {'tp'}, dimensions={1}, use_global_device_ids=true | all-gather | bytes 491520 | tf_op jit(solution)/shard_map/all_gather | solution.py:33
  25.5 0.3 fusion.2
  25.8 0.5 convolution_convert_fusion
  26.3 18.4 %all_to_all.10 = bf16[4,20,6144]{2,1,0:T(8,128)(2,1)S(1)} all-to-all(bf16[4,20,6144]{2,1,0:T(8,128)(2,1)S(1)} %convolution_convert_fusion), channel_id=1, replica_groups=mesh['rep'=2,'exp'=4,'tp'=4] {'exp'}, dimensions={0} | all-to-all | bytes 1966080 | tf_op jit(solution)/shard_map/all_to_all | solution.py:38
  44.7 0.3 reshape.20
  45.0 10.5 %fusion.16 = f32[80,2048]{1,0:T(8,128)S(1)} fusion(bf16[80,6144]{1,0:T(8,128)(2,1)S(1)} %reshape.20, bf16[6144,2048]{1,0:T(8,128)(2,1)} %param.9), kind=kOutput, calls=%fused_computation.31 | convolution fusion | flops 2013265920 | bytes 26804224 | tf_op jit(solution)/shard_map/dot_general | solution.py:40
  55.4 0.0 copy-start.1
  55.4 0.0 copy-start
  55.5 19.9 %convolution_convert_fusion.1 = bf16[80,6144]{1,0:T(8,128)(2,1)S(1)} fusion(bf16[2048,6144]{1,0:T(8,128)(2,1)} %param.11, bf16[80,6144]{1,0:T(8,128)(2,1)S(1)} %reshape.20, bf16[6144,2048]{1,0:T(8,128)(2,1)} %param.10, f32[80,2048]{1,0:T(8,128)S(1)} %fusion.16), kind=kOutput, calls=%fused_computation.1 | convolution fusion | flops 4028006400 | bytes 52953088 | tf_op jit(solution)/shard_map/dot_general | solution.py:43
  75.4 1.1 reshape.21
  76.5 0.0 reduce-scatter.2.cloned.1.call-update
  76.5 0.0 copy-done.1
  76.6 0.0 copy-done
  76.6 0.1 copy.15
  76.7 30.1 %reduce-scatter.2.cloned.1.call-done = bf16[4,20,1536]{2,1,0:T(8,128)(2,1)} async-done(((bf16[4,20,6144]{2,1,0:T(8,128)(2,1)}), bf16[4,20,1536]{2,1,0:T(8,128)(2,1)}) %reduce-scatter.2.cloned.1.call-update) | async-done | bytes 245776 | tf_op jit(solution)/shard_map/reduce_scatter | solution.py:47
  106.9 3.5 %all-to-all-start.1 = ((bf16[4,20,1536]{2,1,0:T(8,128)(2,1)}), bf16[4,20,1536]{2,1,0:T(8,128)(2,1)S(1)}, u32[]{:S(2)}, u32[]{:S(2)}) async-start(bf16[4,20,1536]{2,1,0:T(8,128)(2,1)} %reduce-scatter.2.cloned.1.call-done), calls=%async_computation.2 | async-start | bytes 589824 | tf_op jit(solution)/shard_map/all_to_all | solution.py:53
  110.3 0.3 fusion.12
  110.6 6.1 %all-to-all-done.1 = bf16[4,20,1536]{2,1,0:T(8,128)(2,1)S(1)} async-done(((bf16[4,20,1536]{2,1,0:T(8,128)(2,1)}), bf16[4,20,1536]{2,1,0:T(8,128)(2,1)S(1)}, u32[]{:S(2)}, u32[]{:S(2)}) %all-to-all-start.1) | async-done | bytes 245792 | tf_op jit(solution)/shard_map/all_to_all | solution.py:53
  116.6 1.1 fusion.1
  (4 shorter events, 0.0 us)
Async XLA Ops:
  6.5 100.3 %reduce-scatter.2.cloned.1.call-start = ((), (), s32[]{:S(2)}) async-start(), calls=%async_computation.3 | async-start | bytes 1474560 | tf_op jit(solution)/shard_map/reduce_scatter | solution.py:47
  55.4 21.1 %copy-start.1 = (f32[32,2]{0,1:T(2,128)S(1)}, f32[32,2]{0,1:T(2,128)}, u32[]{:S(2)}) copy-start(f32[32,2]{0,1:T(2,128)} %param.8) | copy-start | bytes 772
  55.4 21.1 %copy-start = (s32[32,2]{0,1:T(2,128)S(1)}, s32[32,2]{0,1:T(2,128)}, u32[]{:S(2)}) copy-start(s32[32,2]{0,1:T(2,128)} %param.7) | copy-start | bytes 772
  106.9 9.8 %all-to-all-start.1 = ((bf16[4,20,1536]{2,1,0:T(8,128)(2,1)}), bf16[4,20,1536]{2,1,0:T(8,128)(2,1)S(1)}, u32[]{:S(2)}, u32[]{:S(2)}) async-start(bf16[4,20,1536]{2,1,0:T(8,128)(2,1)} %reduce-scatter.2.cloned.1.call-done), calls=%async_computation.2 | async-start | bytes 589824 | tf_op jit(solution)/shard_map/all_to_all | solution.py:53
Sparse Core Ops, SparseCore 0:
  76.7 30.1 reduce-scatter.1
where the time goes:
time: 125 us
  waiting for transfers between devices  36.2 us (29%)
  blocking collectives  34.9 us (28%)
  matrix products  32.5 us (26%)
  between operations  13.5 us (11%)
  starting transfers between devices  3.45 us (3%)
  other arithmetic  2.17 us (2%)
  local copies, waits for them, and re-layouts  1.89 us (2%)
    reduce_scatter x1, waiting for transfers between devices, on_device(): lax.psum_scatter(partial_value.astype(jnp.float32).astype(jnp.bfloat16),...  30.1 us
    dot_general x1, matrix products, on_device(): jnp.dot(hidden, down_weight, preferred_element_type=jnp.float32)  19.9 us
    all_to_all x1, blocking collectives, on_device(): lax.all_to_all(outgoing, 'exp', split_axis=0, concat_axis=0, tiled=True)  18.4 us
    all_gather x1, blocking collectives, on_device(): whole_rows = lax.all_gather(tokens, 'tp', axis=1, tiled=True)  16.5 us
    dot_general x1, matrix products, on_device(): jnp.dot(slot_rows, gate_weight, preferred_element_type=jnp.float32)  10.5 us
    all_to_all x1, waiting for transfers between devices, on_device(): lax.all_to_all(narrow.astype(jnp.bfloat16), 'exp', split_axis=0, concat_a...  6.06 us
    all_to_all x1, starting transfers between devices, on_device(): lax.all_to_all(narrow.astype(jnp.bfloat16), 'exp', split_axis=0, concat_a...  3.45 us
  transfers between devices with their start and end apart: 2, of which 2 were waited for; matrix products, arithmetic and copies ran while one was open for 0% of the time, Pallas kernels for 0%

commit v1 on v0

--- a/solution.py
+++ b/solution.py
@@ -30,7 +30,7 @@
     exp_count = lax.axis_size("exp")
     groups = exp_count // EXPERTS
     placement, mixing = slot_tables(expert_ids, route_logits)
-    whole_rows = lax.all_gather(tokens, "tp", axis=1, tiled=True)
+    whole_rows = jnp.concatenate(lax.all_gather(tokens, "tp"), axis=1)
     slots = jnp.einsum(
         "ect,td->ecd", placement, whole_rows, preferred_element_type=jnp.float32
     ).astype(jnp.bfloat16)

time: 125 us -> 125 us (level)
  no operation moved by 1% of the time
where the time goes in v1:
time: 125 us
  waiting for transfers between devices  36.2 us (29%)
  blocking collectives  34.9 us (28%)
  matrix products  32.5 us (26%)
  between operations  13.5 us (11%)
  starting transfers between devices  3.45 us (3%)
  local copies, waits for them, and re-layouts  2.48 us (2%)
  other arithmetic  2.17 us (2%)
    reduce_scatter x1, waiting for transfers between devices, on_device(): lax.psum_scatter(partial_value.astype(jnp.float32).astype(jnp.bfloat16),...  30.1 us
    dot_general x1, matrix products, on_device(): jnp.dot(hidden, down_weight, preferred_element_type=jnp.float32)  19.9 us
    all_to_all x1, blocking collectives, on_device(): lax.all_to_all(outgoing, 'exp', split_axis=0, concat_axis=0, tiled=True)  18.4 us
    all_gather x1, blocking collectives, on_device(): whole_rows = jnp.concatenate(lax.all_gather(tokens, 'tp'), axis=1)  16.5 us
    dot_general x1, matrix products, on_device(): jnp.dot(slot_rows, gate_weight, preferred_element_type=jnp.float32)  10.5 us
    all_to_all x1, waiting for transfers between devices, on_device(): lax.all_to_all(narrow.astype(jnp.bfloat16), 'exp', split_axis=0, concat_a...  6.06 us
    all_to_all x1, starting transfers between devices, on_device(): lax.all_to_all(narrow.astype(jnp.bfloat16), 'exp', split_axis=0, concat_a...  3.45 us
  transfers between devices with their start and end apart: 2, of which 2 were waited for; matrix products, arithmetic and copies ran while one was open for 0% of the time, Pallas kernels for 0%

profile of v1, /device:TPU:0, one launch (start us, length us, event | category | flops | bytes accessed | tf_op | source)
XLA Modules:
  0.0 125.1 jit_solution(4094414334063270027)
XLA Ops:
  6.5 0.0 reduce-scatter.2.cloned.1.call-start
  6.5 0.7 convert_reduce_fusion
  7.2 0.7 convert_convert_fusion
  7.9 0.1 copy.13
  8.0 0.1 reduce_window_sum.11
  8.1 0.1 copy.15
  8.1 0.7 select_reduce_fusion
  8.8 0.1 copy.16
  8.9 0.1 copy.18
  9.0 16.5 %all-gather = bf16[128,1536]{1,0:T(8,128)(2,1)S(1)} all-gather(bf16[32,1536]{1,0:T(8,128)(2,1)} %param.6), channel_id=2, replica_groups=mesh['rep'=2,'exp'=4,'tp'=4] {'tp'}, dimensions={0}, use_global_device_ids=true | all-gather | bytes 491520 | tf_op jit(solution)/shard_map/all_gather | solution.py:33
  25.5 0.3 copy.27
  25.8 0.3 reshape.31
  26.1 0.3 fusion.2
  26.4 0.5 convolution_convert_fusion
  26.9 18.4 %all_to_all.10 = bf16[4,20,6144]{2,1,0:T(8,128)(2,1)S(1)} all-to-all(bf16[4,20,6144]{2,1,0:T(8,128)(2,1)S(1)} %convolution_convert_fusion), channel_id=1, replica_groups=mesh['rep'=2,'exp'=4,'tp'=4] {'exp'}, dimensions={0} | all-to-all | bytes 1966080 | tf_op jit(solution)/shard_map/all_to_all | solution.py:38
  45.3 0.3 reshape.28
  45.6 10.5 %fusion.15 = f32[80,2048]{1,0:T(8,128)S(1)} fusion(bf16[80,6144]{1,0:T(8,128)(2,1)S(1)} %reshape.28, bf16[6144,2048]{1,0:T(8,128)(2,1)} %param.9), kind=kOutput, calls=%fused_computation.31 | convolution fusion | flops 2013265920 | bytes 26804224 | tf_op jit(solution)/shard_map/dot_general | solution.py:40
  56.0 0.0 copy-start.1
  56.0 0.0 copy-start
  56.1 19.9 %convolution_convert_fusion.1 = bf16[80,6144]{1,0:T(8,128)(2,1)S(1)} fusion(bf16[2048,6144]{1,0:T(8,128)(2,1)} %param.11, bf16[80,6144]{1,0:T(8,128)(2,1)S(1)} %reshape.28, bf16[6144,2048]{1,0:T(8,128)(2,1)} %param.10, f32[80,2048]{1,0:T(8,128)S(1)} %fusion.15), kind=kOutput, calls=%fused_computation.1 | convolution fusion | flops 4028006400 | bytes 52953088 | tf_op jit(solution)/shard_map/dot_general | solution.py:43
  76.0 1.1 reshape.29
  77.1 0.0 reduce-scatter.2.cloned.1.call-update
  77.1 0.0 copy-done.1
  77.2 0.0 copy-done
  77.2 0.1 copy.17
  77.3 30.1 %reduce-scatter.2.cloned.1.call-done = bf16[4,20,1536]{2,1,0:T(8,128)(2,1)} async-done(((bf16[4,20,6144]{2,1,0:T(8,128)(2,1)}), bf16[4,20,1536]{2,1,0:T(8,128)(2,1)}) %reduce-scatter.2.cloned.1.call-update) | async-done | bytes 245776 | tf_op jit(solution)/shard_map/reduce_scatter | solution.py:47
  107.4 3.5 %all-to-all-start.1 = ((bf16[4,20,1536]{2,1,0:T(8,128)(2,1)}), bf16[4,20,1536]{2,1,0:T(8,128)(2,1)S(1)}, u32[]{:S(2)}, u32[]{:S(2)}) async-start(bf16[4,20,1536]{2,1,0:T(8,128)(2,1)} %reduce-scatter.2.cloned.1.call-done), calls=%async_computation.2 | async-start | bytes 589824 | tf_op jit(solution)/shard_map/all_to_all | solution.py:53
  110.9 0.3 fusion.11
  111.2 6.1 %all-to-all-done.1 = bf16[4,20,1536]{2,1,0:T(8,128)(2,1)S(1)} async-done(((bf16[4,20,1536]{2,1,0:T(8,128)(2,1)}), bf16[4,20,1536]{2,1,0:T(8,128)(2,1)S(1)}, u32[]{:S(2)}, u32[]{:S(2)}) %all-to-all-start.1) | async-done | bytes 245792 | tf_op jit(solution)/shard_map/all_to_all | solution.py:53
  117.2 1.1 fusion.1
  (4 shorter events, 0.0 us)
Async XLA Ops:
  6.5 100.9 %reduce-scatter.2.cloned.1.call-start = ((), (), s32[]{:S(2)}) async-start(), calls=%async_computation.3 | async-start | bytes 1474560 | tf_op jit(solution)/shard_map/reduce_scatter | solution.py:47
  56.0 21.1 %copy-start.1 = (f32[32,2]{0,1:T(2,128)S(1)}, f32[32,2]{0,1:T(2,128)}, u32[]{:S(2)}) copy-start(f32[32,2]{0,1:T(2,128)} %param.8) | copy-start | bytes 772
  56.0 21.1 %copy-start = (s32[32,2]{0,1:T(2,128)S(1)}, s32[32,2]{0,1:T(2,128)}, u32[]{:S(2)}) copy-start(s32[32,2]{0,1:T(2,128)} %param.7) | copy-start | bytes 772
  107.4 9.8 %all-to-all-start.1 = ((bf16[4,20,1536]{2,1,0:T(8,128)(2,1)}), bf16[4,20,1536]{2,1,0:T(8,128)(2,1)S(1)}, u32[]{:S(2)}, u32[]{:S(2)}) async-start(bf16[4,20,1536]{2,1,0:T(8,128)(2,1)} %reduce-scatter.2.cloned.1.call-done), calls=%async_computation.2 | async-start | bytes 589824 | tf_op jit(solution)/shard_map/all_to_all | solution.py:53
Sparse Core Ops, SparseCore 0:
  77.3 30.1 reduce-scatter.1
